TPU v7x, 128 devices: a whole 4x4x4 slice. The times are simulated.
128 devices in a mesh: rows: 16 (over y, z), trees: 8 (over x, core).
Axes of the slice: x: 4, y: 4, z: 4, core: 2. Of those that a mesh axis runs over, the one named last changes fastest.
Arguments:
- leaf_index: int32 [128, 262144], P(None, ('rows', 'trees')), may hold values from 0 to 31, as said below
- out_of_bag: bfloat16 [128, 262144], P(None, ('rows', 'trees')), may hold values from 0 to 4, as said below
- labels: int32 [262144], P(('rows', 'trees')), may hold values from 0 to 999
Outputs:
- tallies: float32 [128, 32, 1000], P('trees', 'rows')
- tree_error: float32 [128], P('trees')
- forest_error: float32 [], replicated
Inputs may be any that keep to these rules, and one draw needn't show every extreme that they name: `out_of_bag`: 0 exactly where a row was in a tree's sample, else at least 0.25. `leaf_index`: in each tree, the 2048 rows of one device reach every leaf exactly 2048 // 32 times.
All inputs are finite; a program needn't handle non-finite values.
Results may differ from a plain program's by a relative error of at most 0.0003.
Values sent between devices are 32-bit elements; how exact they have to be, the bound alone decides.
No kernel may reach another device: no remote copies, remote signals or barrier semaphores. Data moves between devices by JAX's collectives and lax.ppermute only.
A program may use at most 128 MiB of HBM per device.

v0:
```python
import jax
import jax.numpy as jnp
from jax import lax
from jax.sharding import Mesh
from jax.sharding import PartitionSpec as P

CLASSES = 1000
LEAVES = 32
ROWS = ("rows_0", "rows_1")
TREES = ("trees_0", "trees_1")
ROWS_TREES = ("rows_0", "rows_1", "trees_0", "trees_1")


def in_blocks(shard, dim, peers):
    before, after = (shard.shape[:dim], shard.shape[dim + 1 :])
    return jnp.moveaxis(shard.reshape(*before, peers, -1, *after), dim, 0)


def summed_on_arrival(shard, axis, dim):
    peers = lax.axis_size(axis)
    parts = lax.all_to_all(in_blocks(shard, dim, peers), axis, 0, 0, tiled=True)
    return jnp.sum(parts, axis=0)


def by_axis(shard, axes):
    for axis in axes:
        shard = lax.psum(shard, axis)
    return shard


def count_table(leaves, weights, row_labels, n_rows):
    leaf_block_size = LEAVES // n_rows
    leaf_grid = jnp.arange(LEAVES, dtype=jnp.int32).reshape(n_rows, leaf_block_size)
    class_ids = jnp.arange(CLASSES, dtype=jnp.int32)
    class_onehot = (row_labels[:, None] == class_ids[None, :]).astype(jnp.bfloat16)
    placed = jnp.where(
        leaves[None, :, None, :] == leaf_grid[:, None, :, None],
        weights[None, :, None, :],
        jnp.zeros((), jnp.bfloat16),
    )
    count_grid = jnp.einsum(
        "rtlz,zc->rtlc", placed, class_onehot, preferred_element_type=jnp.float32
    )
    return count_grid.reshape(-1, CLASSES)


def per_device(leaf_index, out_of_bag, labels):
    n_rows = lax.axis_size(ROWS)
    tree_count = lax.axis_size(TREES)
    tree_block = leaf_index.shape[0] // tree_count
    leaf_block_slice = LEAVES // n_rows
    ordered = count_table(leaf_index, out_of_bag, labels, n_rows)
    partial_sum_table = lax.psum_scatter(ordered, ROWS, scatter_dimension=0, tiled=True)
    owned_part = summed_on_arrival(partial_sum_table, TREES, 0)
    tallies = owned_part.reshape(tree_block, leaf_block_slice, CLASSES)
    leaf_total = jnp.sum(tallies, axis=2)
    leaf_top = jnp.max(tallies, axis=2)
    local_wrong = jnp.sum(leaf_total - leaf_top, axis=1)
    local_seen = jnp.sum(leaf_total, axis=1)
    wrong_sum, seen_sum = (by_axis(local_wrong, ROWS), by_axis(local_seen, ROWS))
    tree_error = wrong_sum / seen_sum
    all_wrong, all_seen = (
        by_axis(jnp.sum(local_wrong), ROWS_TREES),
        by_axis(jnp.sum(local_seen), ROWS_TREES),
    )
    forest_error = all_wrong / all_seen
    return (tallies, tree_error, forest_error)


def solution(mesh):
    split = Mesh(mesh.devices.reshape(4, 4, 4, 2), ("rows_0", "rows_1", "trees_0", "trees_1"))
    placed = (P(None, ROWS_TREES), P(None, ROWS_TREES), P(ROWS_TREES))
    return jax.shard_map(
        per_device,
        mesh=split,
        in_specs=placed,
        out_specs=(P(TREES, ROWS, None), P(TREES), P()),
        check_vma=False,
    )
```

profile of v0, /device:TPU:1, one launch (start us, length us, event | category | flops | bytes accessed | tf_op | source)
XLA Modules:
  0.0 254.7 jit_solution(17443909807189443048)
XLA Ops:
  7.2 0.0 reduce-scatter.2.cloned.1.call-start
  7.2 21.7 %fusion = f32[16,128,2,1000]{1,3,2,0:T(8,128)} fusion(s32[16,2]{1,0:T(8,128)S(1)} %multiply_add_fusion, s32[128,2048]{1,0:T(8,128)} %param.3, bf16[128,2048]{1,0:T(8,128)(2,1)} %param.4, s32[2048]{0:T(1024)} %param.5), kind=kOutput, calls=%fused_computation.1 | convolution fusion | flops 16796041216 | bytes 17965184 | tf_op jit(solution)/shard_map/rtlz,zc->rtlc/dot_general | solution.py:41
  29.0 25.1 %copy.6 = f32[16,128,2,1000]{3,2,1,0:T(2,128)} copy(f32[16,128,2,1000]{1,3,2,0:T(8,128)} %fusion) | data formatting | bytes 32768000 | tf_op jit(solution)/shard_map/rtlz,zc->rtlc/dot_general | solution.py:41
  54.0 20.8 %reshape.34 = f32[4096,1000]{1,0:T(8,128)} reshape(f32[16,128,2,1000]{3,2,1,0:T(2,128)} %copy.6) | data formatting | bytes 32768000 | tf_op jit(solution)/shard_map/reshape | solution.py:44
  74.8 0.0 reduce-scatter.2.cloned.1.call-update
  74.8 114.0 %reduce-scatter.2.cloned.1.call-done = f32[256,1000]{1,0:T(8,128)} async-done(((f32[4096,1000]{1,0:T(8,128)}), f32[256,1000]{1,0:T(8,128)}) %reduce-scatter.2.cloned.1.call-update) | async-done | bytes 1024016 | tf_op jit(solution)/shard_map/reduce_scatter | solution.py:53
  188.9 20.1 %all_to_all.5 = f32[8,32,1000]{2,1,0:T(8,128)S(1)} all-to-all(f32[8,32,1000]{2,1,0:T(8,128)} %bitcast.6), channel_id=1, replica_groups=mesh['rows_0'=4,'rows_1'=4,'trees_0'=4,'trees_1'=2] {'trees_0','trees_1'}, dimensions={0} | all-to-all | bytes 2048000 | tf_op jit(solution)/shard_map/all_to_all | solution.py:21
  209.0 0.9 fusion.9
  209.9 0.7 reshape.36
  210.6 0.1 reduce_max.11
  210.7 0.1 reduce_max.12
  210.8 0.6 subtract_reduce_fusion.1
  211.4 0.1 reduce_sum.58
  211.5 0.1 fusion.10
  211.6 8.7 %all-reduce.2 = (f32[16]{0:T(128)S(1)}, f32[16]{0:T(128)S(1)}, f32[]{:T(128)}, f32[]{:T(128)}) all-reduce(f32[16]{0:T(128)S(1)} %get-tuple-element.7, f32[16]{0:T(128)S(1)} %get-tuple-element.6, f32[]{:T(128)} %subtract_reduce_fusion.1, f32[]{:T(128)} %get-tuple-element.3), channel_id=1, replica_groups=mesh['rows_0'=4,'rows_1'=4,'trees_0'=4,'trees_1'=2] {'rows_0'}, use_global_device_ids=true, to_apply=%region_5.6 | all-reduce | flops 34 | bytes 272 | tf_op jit(solution)/shard_map/psum | solution.py:27
  220.3 7.4 %all-reduce.1 = (f32[16]{0:T(128)S(1)}, f32[16]{0:T(128)S(1)}, f32[]{:T(128)}, f32[]{:T(128)}) all-reduce(f32[16]{0:T(128)S(1)} %get-tuple-element.14, f32[16]{0:T(128)S(1)} %get-tuple-element.15, f32[]{:T(128)} %get-tuple-element.16, f32[]{:T(128)} %get-tuple-element.17), channel_id=1, replica_groups=mesh['rows_0'=4,'rows_1'=4,'trees_0'=4,'trees_1'=2] {'rows_1'}, use_global_device_ids=true, to_apply=%region_6.7 | all-reduce | flops 34 | bytes 272 | tf_op jit(solution)/shard_map/psum | solution.py:27
  227.7 0.5 div.6
  228.2 7.6 %all-reduce = (f32[]{:T(128)}, f32[]{:T(128)}) all-reduce(f32[]{:T(128)} %get-tuple-element.12, f32[]{:T(128)} %get-tuple-element.13), channel_id=1, replica_groups=mesh['rows_0'=4,'rows_1'=4,'trees_0'=4,'trees_1'=2] {'trees_0'}, use_global_device_ids=true, to_apply=%region_13.14 | all-reduce | flops 2 | bytes 16 | tf_op jit(solution)/shard_map/psum | solution.py:27
  235.8 9.7 %all-reduce.3 = (f32[]{:T(128)}, f32[]{:T(128)}) all-reduce(f32[]{:T(128)} %get-tuple-element.8, f32[]{:T(128)} %get-tuple-element.9), channel_id=1, replica_groups=mesh['rows_0'=4,'rows_1'=4,'trees_0'=4,'trees_1'=2] {'trees_1'}, use_global_device_ids=true, to_apply=%region_14.15 | all-reduce | flops 2 | bytes 16 | tf_op jit(solution)/shard_map/psum | solution.py:27
  (1 shorter events, 0.0 us)
Async XLA Ops:
  7.2 181.7 %reduce-scatter.2.cloned.1.call-start = ((), (), s32[]{:S(2)}) async-start(), calls=%async_computation.2 | async-start | bytes 17825792 | tf_op jit(solution)/shard_map/reduce_scatter | solution.py:53
Sparse Core Ops, SparseCore 0:
  74.9 113.8 reduce-scatter.1
where the time goes:
time: 256 us; the launch traced here: 255 us
  waiting for transfers between devices  114 us (45%)
  blocking collectives  53.4 us (21%)
  local copies, waits for them, and re-layouts  46.7 us (18%)
  matrix products  21.7 us (8%)
  between operations  16.4 us (6%)
    reduce_scatter x1, waiting for transfers between devices, per_device(): lax.psum_scatter(ordered, ROWS, scatter_dimension=0, tiled=True)  114 us
    psum x4, blocking collectives, by_axis(): shard = lax.psum(shard, axis)  33.3 us
    dot_general x1, local copies, waits for them, and re-layouts, count_table(): jnp.einsum('rtlz,zc->rtlc', placed, class_onehot, preferred_element_type=...  25.1 us
    dot_general x1, matrix products, count_table(): jnp.einsum('rtlz,zc->rtlc', placed, class_onehot, preferred_element_type=...  21.7 us
    reshape x1, local copies, waits for them, and re-layouts, count_table(): return count_grid.reshape(-1, CLASSES)  20.8 us
    all_to_all x1, blocking collectives, summed_on_arrival(): parts = lax.all_to_all(in_blocks(shard, dim, peers), axis, 0, 0, tiled=True)  20.1 us
  transfers between devices with their start and end apart: 1, of which 1 were waited for; matrix products, arithmetic and copies ran while one was open for 0% of the time, Pallas kernels for 0%

commit v1 on v0

v1 whole, which is shorter than its diff:
```python
import functools

import jax
import jax.numpy as jnp
from jax import lax
from jax.experimental import pallas as pl
from jax.experimental.pallas import tpu as pltpu
from jax.sharding import Mesh
from jax.sharding import PartitionSpec as P

CLASSES = 1000
LEAVES = 32
TREES_ALL = 128
ROW_DEV = 2048
N_DEV = 128
N_ROWS = 16
N_TREES = 8
RANKS = ROW_DEV // LEAVES
ROWS = ("rows_0", "rows_1")
TREES = ("trees_0", "trees_1")
ALL = ROWS + TREES

OCT = 8
PAIRS = OCT // 2
CHUNKS = 2
CHUNK_ROWS = PAIRS * 4
BLOCK = 256
N_BLOCK = ROW_DEV // BLOCK
WORDS = 11
VMEM = 56 * 1024 * 1024

F32 = jnp.float32
BF16 = jnp.bfloat16


def iota16(shape):
    return lax.broadcasted_iota(jnp.int32, shape, 0).astype(F32).astype(BF16)


def pack_kernel(half, leaf_ref, oob_ref, lab_ref, out_ref, leaf_s, w_s, rank_s, enc_s):
    lab = lab_ref[...]
    enc = lax.shift_left(128 + (lab & 127), lab >> 7).astype(F32)
    enc_s[...] = jnp.broadcast_to(enc, (16, ROW_DEV)).astype(BF16)
    tri = (
        lax.broadcasted_iota(jnp.int32, (BLOCK, BLOCK), 0)
        <= lax.broadcasted_iota(jnp.int32, (BLOCK, BLOCK), 1)
    ).astype(F32).astype(BF16)
    row16 = iota16((16, ROW_DEV))
    zero = jnp.zeros((16, ROW_DEV), BF16)
    one = jnp.ones((16, ROW_DEV), BF16)
    low = lax.broadcasted_iota(jnp.int32, (LEAVES, 128), 1) < RANKS

    def octet(g, carry):
        leaf = leaf_ref[g, pl.ds(half * OCT, OCT), :]
        w = oob_ref[g, pl.ds(half * OCT, OCT), :].astype(F32)
        word = (leaf * 171) >> 9
        field = leaf - 3 * word
        unit = jnp.where(field == 0, 1.0, jnp.where(field == 1, 128.0, 16384.0))
        held = [jnp.where(word == j, unit, 0.0) for j in range(WORDS)]
        marks = jnp.concatenate(
            [held[j][:, b * BLOCK : (b + 1) * BLOCK] for j in range(WORDS) for b in range(N_BLOCK)],
            axis=0,
        ).astype(BF16)
        counts = jnp.dot(marks, tri, preferred_element_type=F32)
        picked = [jnp.zeros((OCT, BLOCK), F32) for _ in range(N_BLOCK)]
        for j in range(WORDS):
            before = jnp.zeros((OCT, BLOCK), F32)
            for b in range(N_BLOCK):
                at = (j * N_BLOCK + b) * OCT
                here = counts[at : at + OCT]
                mine = word[:, b * BLOCK : (b + 1) * BLOCK] == j
                picked[b] = jnp.where(mine, here + before, picked[b])
                if b + 1 < N_BLOCK:
                    before = before + jnp.broadcast_to(here[:, BLOCK - 1 :], (OCT, BLOCK))
        number = jnp.concatenate(picked, axis=1).astype(jnp.int32)
        rank = ((number >> (7 * field)) & 127) - 1
        leaf_s[...] = leaf.astype(F32)
        w_s[...] = w
        rank_s[...] = rank.astype(F32)
        enc_b = enc_s[...]
        for pair in range(PAIRS):
            placed = []
            for t in (2 * pair, 2 * pair + 1):
                leaf_b = jnp.broadcast_to(leaf_s[t : t + 1, :], (16, ROW_DEV)).astype(BF16)
                w_b = jnp.broadcast_to(w_s[t : t + 1, :], (16, ROW_DEV)).astype(BF16)
                rank_b = jnp.broadcast_to(rank_s[t : t + 1, :], (16, ROW_DEV)).astype(BF16)
                at_leaf = [leaf_b == (row16 + 16 * i) for i in range(2)]
                lhs = jnp.concatenate(
                    [jnp.where(m, w_b, zero) for m in at_leaf] + [jnp.where(m, enc_b, zero) for m in at_leaf],
                    axis=0,
                )
                rhs = jnp.concatenate(
                    [jnp.where(rank_b == (row16 + 16 * i), one, zero) for i in range(4)], axis=0
                )
                placed.append(
                    lax.dot_general(lhs, rhs, (((1,), (1,)), ((), ())), preferred_element_type=F32)
                )
            both = jnp.concatenate(placed, axis=1)
            weights = both[:LEAVES]
            code = both[LEAVES:].astype(jnp.int32)
            high = 24 - lax.clz(code)
            label = ((code >> high) + (high - 1) * 128).astype(F32)
            for p in range(N_ROWS):
                out_ref[p, g, 4 * pair : 4 * pair + 2, :] = weights[2 * p : 2 * p + 2]
                out_ref[p, g, 4 * pair + 2 : 4 * pair + 4, :] = label[2 * p : 2 * p + 2]
        return carry

    lax.fori_loop(0, N_TREES, octet, 0)


def pack(half, leaf_index, out_of_bag, labels):
    return pl.pallas_call(
        functools.partial(pack_kernel, half),
        out_shape=jax.ShapeDtypeStruct((N_ROWS, N_TREES, CHUNK_ROWS, 128), F32),
        scratch_shapes=[
            pltpu.VMEM((OCT, ROW_DEV), F32),
            pltpu.VMEM((OCT, ROW_DEV), F32),
            pltpu.VMEM((OCT, ROW_DEV), F32),
            pltpu.VMEM((16, ROW_DEV), BF16),
        ],
        compiler_params=pltpu.CompilerParams(vmem_limit_bytes=VMEM),
        cost_estimate=pl.CostEstimate(flops=4_000_000_000, bytes_accessed=3_000_000, transcendentals=0),
        name=f"pack_{half}",
    )(
        leaf_index.reshape(N_TREES, 16, ROW_DEV),
        out_of_bag.reshape(N_TREES, 16, ROW_DEV),
        labels.reshape(1, ROW_DEV),
    )


GROUPS = OCT * 2
HALF_DEV = N_DEV // 2


def tally_kernel(in_ref, out_ref, wrong_ref, seen_ref, w_s, hi_s, lo_s):
    low = lax.broadcasted_iota(jnp.int32, (HALF_DEV, 128), 1) < RANKS
    row16 = iota16((16, 128))
    zero = jnp.zeros((16, 128), BF16)
    one = jnp.ones((16, 128), BF16)

    def halves(row):
        a = in_ref[0:HALF_DEV, row, :]
        b = in_ref[HALF_DEV:N_DEV, row, :]
        return (
            jnp.where(low, a, pltpu.roll(b, RANKS, 1)),
            jnp.where(low, pltpu.roll(a, RANKS, 1), b),
        )

    for pair in range(PAIRS):
        for leaf in range(2):
            w2 = halves(4 * pair + leaf)
            lab2 = halves(4 * pair + 2 + leaf)
            for odd in range(2):
                hi = jnp.floor(lab2[odd] * (1.0 / 32.0))
                w_s[...] = w2[odd]
                hi_s[...] = hi
                lo_s[...] = lab2[odd] - 32.0 * hi
                lhs, rhs = [], []
                for r in range(HALF_DEV):
                    w_b = jnp.broadcast_to(w_s[r : r + 1, :], (16, 128)).astype(BF16)
                    hi_b = jnp.broadcast_to(hi_s[r : r + 1, :], (16, 128)).astype(BF16)
                    lo_b = jnp.broadcast_to(lo_s[r : r + 1, :], (16, 128)).astype(BF16)
                    lhs.append(
                        jnp.concatenate([jnp.where(hi_b == row16 + 16 * i, w_b, zero) for i in range(2)], axis=0)
                    )
                    rhs.append(
                        jnp.concatenate([jnp.where(lo_b == row16 + 16 * i, one, zero) for i in range(2)], axis=0)
                    )
                table = lax.dot_general(
                    jnp.concatenate(lhs, axis=1),
                    jnp.concatenate(rhs, axis=1),
                    (((1,), (1,)), ((), ())),
                    preferred_element_type=F32,
                )
                group = (2 * pair + odd) * 2 + leaf
                out_ref[group] = table
                total = jnp.sum(jnp.sum(table, axis=0, keepdims=True), axis=1, keepdims=True)
                top = jnp.max(jnp.max(table, axis=0, keepdims=True), axis=1, keepdims=True)
                seen_ref[group : group + 1, :] = jnp.broadcast_to(total, (1, 128))
                wrong_ref[group : group + 1, :] = jnp.broadcast_to(total - top, (1, 128))


def tally(received):
    return pl.pallas_call(
        tally_kernel,
        out_shape=(
            jax.ShapeDtypeStruct((GROUPS, 32, 32), F32),
            jax.ShapeDtypeStruct((GROUPS, 128), F32),
            jax.ShapeDtypeStruct((GROUPS, 128), F32),
        ),
        scratch_shapes=[pltpu.VMEM((HALF_DEV, 128), F32)] * 3,
        compiler_params=pltpu.CompilerParams(vmem_limit_bytes=VMEM),
        cost_estimate=pl.CostEstimate(flops=2_000_000_000, bytes_accessed=2_000_000, transcendentals=0),
        name="tally",
    )(received)


def per_device(leaf_index, out_of_bag, labels):
    tables, wrongs, seens = [], [], []
    sent = []
    for half in range(CHUNKS):
        packed = pack(half, leaf_index, out_of_bag, labels)
        packed = packed.reshape(N_DEV, CHUNK_ROWS, 128)
        sent.append(lax.all_to_all(packed, ALL, 0, 0, tiled=True))
    for part in sent:
        table, wrong, seen = tally(part)
        tables.append(table.reshape(OCT, 2, 1024)[:, :, :CLASSES])
        wrongs.append(wrong[:, 0].reshape(OCT, 2).sum(1))
        seens.append(seen[:, 0].reshape(OCT, 2).sum(1))
    wrong = jnp.concatenate(wrongs)
    seen = jnp.concatenate(seens)
    mine = (jnp.arange(N_DEV, dtype=jnp.int32) % N_TREES == lax.axis_index(TREES))[:, None]
    per_tree = jnp.concatenate([wrong, seen])
    pooled = jnp.stack([jnp.sum(wrong), jnp.sum(seen)])
    message = jnp.concatenate(
        [
            jnp.where(mine, per_tree[None, :], 0.0),
            jnp.broadcast_to(pooled[None, :], (N_DEV, 2)),
            jnp.zeros((N_DEV, 94), F32),
        ],
        axis=1,
    )
    sums = jnp.sum(lax.all_to_all(message, ALL, 0, 0, tiled=True), axis=0)
    tree_error = sums[0:16] / sums[16:32]
    forest_error = sums[32] / sums[33]
    return jnp.concatenate(tables, axis=0), tree_error, forest_error


def solution(mesh):
    split = Mesh(mesh.devices.reshape(4, 4, 4, 2), ALL)
    return jax.shard_map(
        per_device,
        mesh=split,
        in_specs=(P(None, ALL), P(None, ALL), P(ALL)),
        out_specs=(P(TREES, ROWS, None), P(TREES), P()),
        check_vma=False,
    )
```

time: 256 us -> 99.6 us (0.39)
  waiting for transfers between devices: 114 us -> 27 us
  blocking collectives: 53.4 us -> 0 us
  local copies, waits for them, and re-layouts: 46.7 us -> 5.36 us
  Pallas kernels: 0 us -> 36.3 us
  matrix products: 21.7 us -> 0 us
  starting transfers between devices: 0.04 us -> 20.3 us
  between operations: 16.4 us -> 5.88 us
    reduce_scatter x1 -> x0, waiting for transfers between devices: 114 us -> none  [per_device(): lax.psum_scatter(ordered, ROWS, scatter_dimension=0, tiled=True)]
    pallas_call x0 -> x4, Pallas kernels: none -> 36.3 us  [the longest x2 25.9 us: pack(): pl.pallas_call(functools.partial(pack_kernel, half), out_shape=jax.ShapeD...]
    psum x4 -> x0, blocking collectives: 33.3 us -> none  [by_axis(): shard = lax.psum(shard, axis)]
    all_to_all x0 -> x3, waiting for transfers between devices: none -> 27 us  [the longest x2 18.1 us: per_device(): sent.append(lax.all_to_all(packed, ALL, 0, 0, tiled=True))]
    dot_general x1 -> x0, local copies, waits for them, and re-layouts: 25.1 us -> none  [count_table(): jnp.einsum('rtlz,zc->rtlc', placed, class_onehot, preferred_element_type=...]
    dot_general x1 -> x0, matrix products: 21.7 us -> none  [count_table(): jnp.einsum('rtlz,zc->rtlc', placed, class_onehot, preferred_element_type=...]
    all_to_all x0 -> x3, starting transfers between devices: none -> 20.3 us  [the longest x2 15.9 us: per_device(): sent.append(lax.all_to_all(packed, ALL, 0, 0, tiled=True))]
    all_to_all x1 -> x0, blocking collectives: 20.1 us -> none  [summed_on_arrival(): parts = lax.all_to_all(in_blocks(shard, dim, peers), axis, 0, 0, tiled=True)]
  transfers between devices with their start and end apart: 1 -> 3, of which waited for: 1 -> 3; matrix products, arithmetic and copies ran while one was open for 0% -> 3% of each run, Pallas kernels for 0% -> 18%
where the time goes in v1:
time: 99.6 us; the launch traced here: 99.1 us
  Pallas kernels  36.3 us (36%)
  waiting for transfers between devices  27 us (27%)
  starting transfers between devices  20.3 us (20%)
  between operations  5.88 us (6%)
  local copies, waits for them, and re-layouts  5.36 us (5%)
  other arithmetic  4.21 us (4%)
    pallas_call x2, Pallas kernels, pack(): pl.pallas_call(functools.partial(pack_kernel, half), out_shape=jax.ShapeD...  25.9 us
    all_to_all x2, waiting for transfers between devices, per_device(): sent.append(lax.all_to_all(packed, ALL, 0, 0, tiled=True))  18.1 us
    all_to_all x2, starting transfers between devices, per_device(): sent.append(lax.all_to_all(packed, ALL, 0, 0, tiled=True))  15.9 us
    pallas_call x2, Pallas kernels, tally(): pl.pallas_call(tally_kernel, out_shape=(jax.ShapeDtypeStruct((GROUPS, 32,...  10.3 us
    all_to_all x1, waiting for transfers between devices, per_device(): sums = jnp.sum(lax.all_to_all(message, ALL, 0, 0, tiled=True), axis=0)  8.89 us
    all_to_all x1, starting transfers between devices, per_device(): sums = jnp.sum(lax.all_to_all(message, ALL, 0, 0, tiled=True), axis=0)  4.43 us
    reshape x2, local copies, waits for them, and re-layouts, per_device(): tables.append(table.reshape(OCT, 2, 1024)[:, :, :CLASSES])  2.27 us
    unnamed x12, local copies, waits for them, and re-layouts  2.04 us
  transfers between devices with their start and end apart: 3, of which 3 were waited for; matrix products, arithmetic and copies ran while one was open for 3% of the time, Pallas kernels for 18%

profile of v1, /device:TPU:1, one launch (start us, length us, event | category | flops | bytes accessed | tf_op | source)
XLA Modules:
  0.0 99.1 jit_solution(4191429505541437232)
XLA Ops:
  0.6 13.0 %pack_1.1 = f32[16,8,16,128]{3,2,1,0:T(8,128)} custom-call(s32[8,16,2048]{2,1,0:T(8,128)} %bitcast.15, bf16[8,16,2048]{2,1,0:T(8,128)(2,1)} %bitcast.17, s32[1,2048]{1,0:T(1,128)} %bitcast.19), custom_call_target="tpu_custom_call" | custom-call | flops 4000000000 | bytes 3000000 | tf_op jit(solution)/shard_map/pack_1/pallas_call | solution.py:112
  13.6 11.5 %all-to-all-start.1 = ((f32[128,16,128]{2,1,0:T(8,128)}), f32[128,16,128]{2,1,0:T(8,128)S(1)}, u32[]{:S(2)}, u32[]{:S(2)}) async-start(f32[128,16,128]{2,1,0:T(8,128)} %bitcast.12), calls=%async_computation.1 | async-start | bytes 2097152 | tf_op jit(solution)/shard_map/all_to_all | solution.py:204
  25.1 12.9 %pack_0.1 = f32[16,8,16,128]{3,2,1,0:T(8,128)} custom-call(s32[8,16,2048]{2,1,0:T(8,128)} %bitcast.16, bf16[8,16,2048]{2,1,0:T(8,128)(2,1)} %bitcast.18, s32[1,2048]{1,0:T(1,128)} %bitcast.20), custom_call_target="tpu_custom_call" | custom-call | flops 4000000000 | bytes 3000000 | tf_op jit(solution)/shard_map/pack_0/pallas_call | solution.py:112
  38.1 6.3 %all-to-all-done.1.in_ref = f32[128,16,128]{2,1,0:T(8,128)S(1)} async-done(((f32[128,16,128]{2,1,0:T(8,128)}), f32[128,16,128]{2,1,0:T(8,128)S(1)}, u32[]{:S(2)}, u32[]{:S(2)}) %all-to-all-start.1) | async-done | bytes 1048608 | tf_op jit(solution)/shard_map/all_to_all | solution.py:204
  44.3 1.0 %copy-done.1 = f32[128,16,128]{2,1,0:T(8,128)} copy-done((f32[128,16,128]{2,1,0:T(8,128)}, f32[128,16,128]{2,1,0:T(8,128)S(1)}, u32[]{:S(2)}) %copy-start.1) | copy-done | bytes 1048600
  45.4 4.4 %all-to-all-start = ((f32[128,16,128]{2,1,0:T(8,128)}), f32[128,16,128]{2,1,0:T(8,128)S(1)}, u32[]{:S(2)}, u32[]{:S(2)}) async-start(f32[128,16,128]{2,1,0:T(8,128)} %bitcast.11), calls=%async_computation | async-start | bytes 2097152 | tf_op jit(solution)/shard_map/all_to_all | solution.py:204
  49.8 0.1 pad.2.clone
  49.9 5.2 %tally.3 = (f32[16,32,32]{2,1,0:T(8,128)}, f32[16,128]{1,0:T(8,128)}, f32[16,128]{1,0:T(8,128)}) custom-call(f32[128,16,128]{2,1,0:T(8,128)} %copy-done.1), custom_call_target="tpu_custom_call" | custom-call | flops 2000000000 | bytes 2000000 | tf_op jit(solution)/shard_map/tally/pallas_call | solution.py:184
  55.1 1.1 %reshape.51 = f32[8,2,1024]{2,1,0:T(2,128)S(1)} reshape(f32[16,32,32]{2,1,0:T(8,128)} %get-tuple-element.10) | data formatting | bytes 131072 | tf_op jit(solution)/shard_map/reshape | solution.py:207
  56.2 0.7 slice_reduce_fusion
  56.9 0.1 reshape_squeeze.15
  57.0 0.1 reduce_sum.82
  57.1 0.1 reshape_squeeze.13
  57.2 0.1 reduce_sum.80
  57.3 11.8 %all-to-all-done.in_ref = f32[128,16,128]{2,1,0:T(8,128)S(1)} async-done(((f32[128,16,128]{2,1,0:T(8,128)}), f32[128,16,128]{2,1,0:T(8,128)S(1)}, u32[]{:S(2)}, u32[]{:S(2)}) %all-to-all-start) | async-done | bytes 1048608 | tf_op jit(solution)/shard_map/all_to_all | solution.py:204
  69.1 1.0 copy-done
  70.1 5.2 %tally.2 = (f32[16,32,32]{2,1,0:T(8,128)}, f32[16,128]{1,0:T(8,128)}, f32[16,128]{1,0:T(8,128)}) custom-call(f32[128,16,128]{2,1,0:T(8,128)} %copy-done), custom_call_target="tpu_custom_call" | custom-call | flops 2000000000 | bytes 2000000 | tf_op jit(solution)/shard_map/tally/pallas_call | solution.py:184
  75.3 1.1 %reshape.49 = f32[8,2,1024]{2,1,0:T(2,128)S(1)} reshape(f32[16,32,32]{2,1,0:T(8,128)} %get-tuple-element.9) | data formatting | bytes 131072 | tf_op jit(solution)/shard_map/reshape | solution.py:207
  76.5 0.7 slice_reduce_fusion.2
  77.2 0.1 reshape_squeeze.14
  77.3 0.1 reduce_sum.81
  77.4 0.1 reshape_squeeze.12
  77.5 0.1 reduce_sum.79
  80.3 0.1 pad_maximum_fusion.2
  80.4 0.1 broadcast_select_fusion
  80.5 0.6 maximum_maximum_fusion
  81.1 4.4 %all-to-all-start.2 = ((f32[128,1,128]{2,1,0:T(1,128)}), f32[128,1,128]{2,1,0:T(1,128)S(1)}, u32[]{:S(2)}, u32[]{:S(2)}) async-start(f32[128,1,128]{2,1,0:T(1,128)} %bitcast.7), calls=%async_computation.2 | async-start | bytes 131072 | tf_op jit(solution)/shard_map/all_to_all | solution.py:223
  85.5 0.7 pad_maximum_fusion
  86.3 8.9 %all-to-all-done.2 = f32[128,1,128]{2,1,0:T(1,128)S(1)} async-done(((f32[128,1,128]{2,1,0:T(1,128)}), f32[128,1,128]{2,1,0:T(1,128)S(1)}, u32[]{:S(2)}, u32[]{:S(2)}) %all-to-all-start.2) | async-done | bytes 65568 | tf_op jit(solution)/shard_map/all_to_all | solution.py:223
  95.2 0.2 reduce_sum.89
  95.3 0.6 slice_divide_fusion
  95.9 0.7 fusion.1
  (13 shorter events, 0.1 us)
Async XLA Ops:
  13.6 30.7 %all-to-all-start.1 = ((f32[128,16,128]{2,1,0:T(8,128)}), f32[128,16,128]{2,1,0:T(8,128)S(1)}, u32[]{:S(2)}, u32[]{:S(2)}) async-start(f32[128,16,128]{2,1,0:T(8,128)} %bitcast.12), calls=%async_computation.1 | async-start | bytes 2097152 | tf_op jit(solution)/shard_map/all_to_all | solution.py:204
  44.3 1.0 %copy-start.1 = (f32[128,16,128]{2,1,0:T(8,128)}, f32[128,16,128]{2,1,0:T(8,128)S(1)}, u32[]{:S(2)}) copy-start(f32[128,16,128]{2,1,0:T(8,128)S(1)} %all-to-all-done.1.in_ref) | copy-start | bytes 3145732
  45.4 23.8 %all-to-all-start = ((f32[128,16,128]{2,1,0:T(8,128)}), f32[128,16,128]{2,1,0:T(8,128)S(1)}, u32[]{:S(2)}, u32[]{:S(2)}) async-start(f32[128,16,128]{2,1,0:T(8,128)} %bitcast.11), calls=%async_computation | async-start | bytes 2097152 | tf_op jit(solution)/shard_map/all_to_all | solution.py:204
  55.1 1.1 %copy-start.2 = (f32[16,128]{1,0:T(8,128)S(1)}, f32[16,128]{1,0:T(8,128)}, u32[]{:S(2)}) copy-start(f32[16,128]{1,0:T(8,128)} %get-tuple-element.12) | copy-start | bytes 24580
  55.1 1.2 %copy-start.3 = (f32[16,128]{1,0:T(8,128)S(1)}, f32[16,128]{1,0:T(8,128)}, u32[]{:S(2)}) copy-start(f32[16,128]{1,0:T(8,128)} %get-tuple-element.14) | copy-start | bytes 24580
  69.1 1.0 copy-start
  75.3 1.1 %copy-start.4 = (f32[16,128]{1,0:T(8,128)S(1)}, f32[16,128]{1,0:T(8,128)}, u32[]{:S(2)}) copy-start(f32[16,128]{1,0:T(8,128)} %get-tuple-element.11) | copy-start | bytes 24580
  75.3 1.2 %copy-start.5 = (f32[16,128]{1,0:T(8,128)S(1)}, f32[16,128]{1,0:T(8,128)}, u32[]{:S(2)}) copy-start(f32[16,128]{1,0:T(8,128)} %get-tuple-element.13) | copy-start | bytes 24580
  81.1 14.0 %all-to-all-start.2 = ((f32[128,1,128]{2,1,0:T(1,128)}), f32[128,1,128]{2,1,0:T(1,128)S(1)}, u32[]{:S(2)}, u32[]{:S(2)}) async-start(f32[128,1,128]{2,1,0:T(1,128)} %bitcast.7), calls=%async_computation.2 | async-start | bytes 131072 | tf_op jit(solution)/shard_map/all_to_all | solution.py:223

commit v2 on v0

v2 whole, which is shorter than its diff:
```python
import jax
import jax.numpy as jnp
from jax import lax
from jax.experimental import pallas as pl
from jax.experimental.pallas import tpu as pltpu
from jax.sharding import Mesh
from jax.sharding import PartitionSpec as P

CLASSES = 1000
LEAVES = 32
TREES_ALL = 128
ROW_DEV = 2048
N_DEV = 128
N_ROWS = 16
N_TREES = 8
GROUP = TREES_ALL // N_TREES
RANKS = ROW_DEV // LEAVES
ROWS = ("rows_0", "rows_1")
TREES = ("trees_0", "trees_1")
ALL = ROWS + TREES
REGS = ROW_DEV // 8
HALF_DEV = N_DEV // 2

F32 = jnp.float32
BF16 = jnp.bfloat16
I32 = jnp.int32


def ordered(x, i, j):
    x[i], x[j] = jnp.minimum(x[i], x[j]), jnp.maximum(x[i], x[j])


COPIES = 4
SPAN = ROW_DEV // COPIES
LEAF_STEP = float(1 << 20)


def pack_kernel(leaf_hbm, oob_hbm, lab_ref, out_hbm, s_ref, leaf_ref, oob_ref, out_ref, leaf_sem, oob_sem, out_sem):
    sub = lax.broadcasted_iota(I32, (8, 128), 0)

    def loads(c):
        cols = pl.ds(c * SPAN, SPAN)
        return (
            pltpu.make_async_copy(leaf_hbm.at[:, cols], leaf_ref.at[c], leaf_sem.at[c]),
            pltpu.make_async_copy(oob_hbm.at[:, cols], oob_ref.at[c], oob_sem.at[c]),
        )

    for c in range(COPIES):
        for copy in loads(c):
            copy.start()

    def get(v):
        return s_ref[pl.ds(pl.multiple_of(v * 8, 8), 8), :]

    def put(v, x):
        s_ref[pl.ds(pl.multiple_of(v * 8, 8), 8), :] = x

    def sort_32(b, carry):
        x = [get(b * 32 + r) for r in range(32)]
        for k in range(1, 6):
            for i in range(32):
                j = i ^ ((1 << k) - 1)
                if i < j:
                    ordered(x, i, j)
            for d in reversed(range(k - 1)):
                for i in range(32):
                    if not i & (1 << d):
                        ordered(x, i, i | (1 << d))
        for r in range(32):
            put(b * 32 + r, x[r])
        return carry

    for c in range(COPIES):
        for copy in loads(c):
            copy.wait()
        for q in range(SPAN // 128):
            cols = pl.ds(q * 128, 128)
            w = oob_ref[c, :, cols].astype(F32) * 512.0
            code = jnp.minimum(
                jnp.minimum(w, w * 0.5 + 128.0), jnp.minimum(w * 0.25 + 256.0, w * 0.125 + 384.0)
            )
            high = (leaf_ref[c, :, cols] - 16).astype(F32) * LEAF_STEP
            label = lab_ref[:, pl.ds(c * SPAN + q * 128, 128)].astype(F32)
            key = high + (code * 1024.0 + label)
            s_ref[pl.ds(c * SPAN + q * 128, 128), :] = jnp.transpose(key)
        lax.fori_loop(c * SPAN // 256, (c + 1) * SPAN // 256, sort_32, 0)

    def low_bits(b, carry):
        x = [get(b * 32 + r) for r in range(32)]
        for d in reversed(range(5)):
            for i in range(32):
                if not i & (1 << d):
                    ordered(x, i, i | (1 << d))
        for r in range(32):
            put(b * 32 + r, x[r])
        return carry

    def swapped(x, flip):
        return jnp.take_along_axis(x, sub ^ flip, axis=0, mode="promise_in_bounds")

    def across(x, y, bit):
        return jnp.where(sub & bit == 0, jnp.minimum(x, y), jnp.maximum(x, y))

    def high_bits(k):
        top = min(k, 8)
        bits = list(range(5, top))
        n = 1 << len(bits)
        per_block = 16
        blocks = REGS >> top

        def body(t, carry):
            block, low = t // per_block, t % per_block
            base = block << top
            at = [base + (h << 5) + low for h in range(n)] + [base + (h << 5) + (31 - low) for h in range(n)]
            x = [get(v) for v in at]
            mirror = lambda e: (n - 1 - e % n) + (n if e < n else 0)
            if k <= 8:
                for e in range(n):
                    if e & (n >> 1):
                        continue
                    ordered(x, e, mirror(e))
                    ordered(x, e + n, mirror(e + n))
            else:
                flip = (1 << (k - 8)) - 1
                x = [across(x[e], swapped(x[mirror(e)], flip), 1 << (k - 9)) for e in range(2 * n)]
                for d in reversed(range(k - 9)):
                    x = [across(v, swapped(v, 1 << d), 1 << d) for v in x]
            first = len(bits) - 2 if k <= 8 else len(bits) - 1
            for d in reversed(range(first + 1)):
                for e in range(2 * n):
                    if not e & (1 << d):
                        ordered(x, e, e | (1 << d))
            for v, val in zip(at, x):
                put(v, val)
            return carry

        lax.fori_loop(0, blocks * per_block, body, 0, unroll=UNROLL[k])

    for k in range(6, 12):
        high_bits(k)
        lax.fori_loop(0, REGS // 32, low_bits, 0)

    def stored(p):
        return pltpu.make_async_copy(out_ref.at[p], out_hbm.at[p], out_sem.at[p])

    odd = (lax.broadcasted_iota(I32, (1, 128), 1) >= RANKS).astype(F32)
    for p in range(N_ROWS):
        start = (p % 2) * 1024 + p // 2
        key = jnp.transpose(s_ref[pl.ds(start, 128, stride=8), :])
        rest = key - (odd + float(2 * p - 16)) * LEAF_STEP
        code = jnp.floor(rest * (1.0 / 1024.0))
        label = rest - code * 1024.0
        w = jnp.maximum(
            jnp.maximum(code, code * 2.0 - 256.0), jnp.maximum(code * 4.0 - 1024.0, code * 8.0 - 3072.0)
        ) * (1.0 / 512.0)
        out_ref[p, :, 0] = w.reshape(N_TREES, GROUP, 128)
        out_ref[p, :, 1] = label.reshape(N_TREES, GROUP, 128)
        stored(p).start()
    for p in range(N_ROWS):
        stored(p).wait()


UNROLL = {6: 4, 7: 2, 8: 1, 9: 1, 10: 1, 11: 1}


def pack(leaf_index, out_of_bag, labels):
    return pl.pallas_call(
        pack_kernel,
        in_specs=[
            pl.BlockSpec(memory_space=pltpu.HBM),
            pl.BlockSpec(memory_space=pltpu.HBM),
            pl.BlockSpec(memory_space=pltpu.VMEM),
        ],
        out_specs=pl.BlockSpec(memory_space=pltpu.HBM),
        out_shape=jax.ShapeDtypeStruct((N_ROWS, N_TREES, 2, GROUP, 128), F32),
        scratch_shapes=[
            pltpu.VMEM((ROW_DEV, 128), F32),
            pltpu.VMEM((COPIES, TREES_ALL, SPAN), I32),
            pltpu.VMEM((COPIES, TREES_ALL, SPAN), BF16),
            pltpu.VMEM((N_ROWS, N_TREES, 2, GROUP, 128), F32),
            pltpu.SemaphoreType.DMA((COPIES,)),
            pltpu.SemaphoreType.DMA((COPIES,)),
            pltpu.SemaphoreType.DMA((N_ROWS,)),
        ],
        compiler_params=pltpu.CompilerParams(vmem_limit_bytes=60 * 1024 * 1024),
        cost_estimate=pl.CostEstimate(flops=40_000_000, bytes_accessed=3_700_000, transcendentals=0),
        name="pack",
    )(leaf_index, out_of_bag, labels.reshape(1, ROW_DEV))


def iota16(shape):
    return lax.broadcasted_iota(I32, shape, 0).astype(F32).astype(BF16)


def tally_kernel(in_ref, table_ref, message_ref, w_s, hi_s, lo_s, sum_s, top_s):
    low16 = lax.broadcasted_iota(I32, (GROUP, 128), 1) < RANKS
    row16 = iota16((16, 128))
    zero = jnp.zeros((16, 128), BF16)
    one = jnp.ones((16, 128), BF16)

    def halves(a, b):
        return (
            jnp.where(low16, a, pltpu.roll(b, RANKS, 1)),
            jnp.where(low16, pltpu.roll(a, RANKS, 1), b),
        )

    def spread(s, carry):
        w2 = halves(in_ref[s, 0], in_ref[s + HALF_DEV, 0])
        lab2 = halves(in_ref[s, 1], in_ref[s + HALF_DEV, 1])
        for leaf in range(2):
            hi = jnp.floor(lab2[leaf] * (1.0 / 32.0))
            w_s[leaf, s] = w2[leaf]
            hi_s[leaf, s] = hi
            lo_s[leaf, s] = lab2[leaf] - 32.0 * hi
        return carry

    lax.fori_loop(0, HALF_DEV, spread, 0, unroll=4)

    def tree(t, carry):
        for leaf in range(2):
            lhs, rhs = [], []
            for r in range(HALF_DEV):
                w_b = jnp.broadcast_to(w_s[leaf, r, pl.ds(t, 1), :], (16, 128)).astype(BF16)
                hi_b = jnp.broadcast_to(hi_s[leaf, r, pl.ds(t, 1), :], (16, 128)).astype(BF16)
                lo_b = jnp.broadcast_to(lo_s[leaf, r, pl.ds(t, 1), :], (16, 128)).astype(BF16)
                lhs.append(jnp.concatenate([jnp.where(hi_b == row16 + 16 * i, w_b, zero) for i in range(2)], axis=0))
                rhs.append(jnp.concatenate([jnp.where(lo_b == row16 + 16 * i, one, zero) for i in range(2)], axis=0))
            table = lax.dot_general(
                jnp.concatenate(lhs, axis=1),
                jnp.concatenate(rhs, axis=1),
                (((1,), (1,)), ((), ())),
                preferred_element_type=F32,
            )
            table_ref[leaf, t] = table
            sum_s[leaf, pl.ds(t, 1), :] = jnp.sum(table, axis=0, keepdims=True)
            top_s[leaf, pl.ds(t, 1), :] = jnp.max(table, axis=0, keepdims=True)
        return carry

    lax.fori_loop(0, GROUP, tree, 0, unroll=4)
    seen = jnp.zeros((GROUP, 1), F32)
    wrong = jnp.zeros((GROUP, 1), F32)
    for leaf in range(2):
        total = jnp.sum(sum_s[leaf], axis=1, keepdims=True)
        seen = seen + total
        wrong = wrong + (total - jnp.max(top_s[leaf], axis=1, keepdims=True))
    lane = lax.broadcasted_iota(I32, (GROUP, 128), 1)
    row = lax.broadcasted_iota(I32, (GROUP, 128), 0)
    placed = jnp.where(lane == row, wrong, 0.0) + jnp.where(lane == row + GROUP, seen, 0.0)
    message_ref[...] = jnp.broadcast_to(jnp.sum(placed, axis=0, keepdims=True), (N_DEV, 128))


def tally(received):
    return pl.pallas_call(
        tally_kernel,
        out_shape=(
            jax.ShapeDtypeStruct((2, GROUP, 32, 32), F32),
            jax.ShapeDtypeStruct((N_DEV, 128), F32),
        ),
        scratch_shapes=[pltpu.VMEM((2, HALF_DEV, GROUP, 128), F32)] * 3 + [pltpu.VMEM((2, GROUP, 32), F32)] * 2,
        compiler_params=pltpu.CompilerParams(vmem_limit_bytes=16 * 1024 * 1024),
        cost_estimate=pl.CostEstimate(flops=4_000_000_000, bytes_accessed=2_500_000, transcendentals=0),
        name="tally",
    )(received)


def errors_kernel(group_ref, in_ref, tree_ref, forest_ref):
    got = in_ref[...]
    source = lax.broadcasted_iota(I32, (N_DEV, 128), 0)
    mine = jnp.sum(jnp.where(source % N_TREES == group_ref[0], got, 0.0), axis=0, keepdims=True)
    every = jnp.sum(got, axis=0, keepdims=True)
    lane = lax.broadcasted_iota(I32, (1, 128), 1)
    wrong = jnp.sum(jnp.where(lane < GROUP, every, 0.0), axis=1, keepdims=True)
    seen = jnp.sum(jnp.where((lane >= GROUP) & (lane < 2 * GROUP), every, 0.0), axis=1, keepdims=True)
    ratio = mine / pltpu.roll(mine, 128 - GROUP, 1)
    tree_ref[...] = ratio[:, :GROUP]
    forest_ref[...] = wrong / seen


def errors(group, received):
    return pl.pallas_call(
        errors_kernel,
        in_specs=[pl.BlockSpec(memory_space=pltpu.SMEM), pl.BlockSpec(memory_space=pltpu.VMEM)],
        out_shape=(
            jax.ShapeDtypeStruct((1, GROUP), F32),
            jax.ShapeDtypeStruct((1, 1), F32),
        ),
        compiler_params=pltpu.CompilerParams(vmem_limit_bytes=4 * 1024 * 1024),
        name="errors",
    )(group, received)


def per_device(leaf_index, out_of_bag, labels):
    packed = pack(leaf_index, out_of_bag, labels).reshape(N_DEV, 2, GROUP, 128)
    received = lax.all_to_all(packed, ALL, 0, 0, tiled=True)
    table, message = tally(received)
    sums = lax.all_to_all(message, ALL, 0, 0, tiled=True)
    group = lax.axis_index(TREES).astype(I32).reshape(1)
    tree_error, forest_error = errors(group, sums)
    tallies = jnp.swapaxes(table.reshape(2, GROUP, 1024), 0, 1)[:, :, :CLASSES]
    return tallies, tree_error.reshape(GROUP), forest_error.reshape(())


def solution(mesh):
    split = Mesh(mesh.devices.reshape(4, 4, 4, 2), ALL)
    return jax.shard_map(
        per_device,
        mesh=split,
        in_specs=(P(None, ALL), P(None, ALL), P(ALL)),
        out_specs=(P(TREES, ROWS, None), P(TREES), P()),
        check_vma=False,
    )
```

time: 256 us -> 74.2 us (0.29)
  waiting for transfers between devices: 114 us -> 8.6 us
  local copies, waits for them, and re-layouts: 46.7 us -> 0.99 us
  matrix products: 21.7 us -> 0 us
  Pallas kernels: 0 us -> 17.4 us
  between operations: 16.4 us -> 0.66 us
  blocking collectives: 53.4 us -> 42 us
  starting transfers between devices: 0.04 us -> 4.38 us
    reduce_scatter x1 -> x0, waiting for transfers between devices: 114 us -> none  [per_device(): lax.psum_scatter(ordered, ROWS, scatter_dimension=0, tiled=True)]
    psum x4 -> x0, blocking collectives: 33.3 us -> none  [by_axis(): shard = lax.psum(shard, axis)]
    dot_general x1 -> x0, local copies, waits for them, and re-layouts: 25.1 us -> none  [count_table(): jnp.einsum('rtlz,zc->rtlc', placed, class_onehot, preferred_element_type=...]
    all_to_all x1, blocking collectives: 20.1 us -> 42 us  [per_device(): received = lax.all_to_all(packed, ALL, 0, 0, tiled=True)]
    dot_general x1 -> x0, matrix products: 21.7 us -> none  [count_table(): jnp.einsum('rtlz,zc->rtlc', placed, class_onehot, preferred_element_type=...]
    reshape x2, local copies, waits for them, and re-layouts: 21.5 us -> 0.99 us  [per_device(): tallies = jnp.swapaxes(table.reshape(2, GROUP, 1024), 0, 1)[:, :, :CLASSES]]
    pallas_call x0 -> x3, Pallas kernels: none -> 17.4 us  [the longest x1 9.42 us: pack(): pl.pallas_call(pack_kernel, in_specs=[pl.BlockSpec(memory_space=pltpu.HBM...]
    all_to_all x0 -> x1, waiting for transfers between devices: none -> 8.6 us  [per_device(): sums = lax.all_to_all(message, ALL, 0, 0, tiled=True)]
  transfers between devices with their start and end apart: 1 -> 1, of which waited for: 1 -> 1; matrix products, arithmetic and copies ran while one was open for 0% -> 1% of each run, Pallas kernels for 0% -> 0%
where the time goes in v2:
time: 74.2 us; the launch traced here: 74 us
  blocking collectives  42 us (57%)
  Pallas kernels  17.4 us (23%)
  waiting for transfers between devices  8.6 us (12%)
  starting transfers between devices  4.38 us (6%)
  local copies, waits for them, and re-layouts  0.99 us (1%)
    all_to_all x1, blocking collectives, per_device(): received = lax.all_to_all(packed, ALL, 0, 0, tiled=True)  42 us
    pallas_call x1, Pallas kernels, pack(): pl.pallas_call(pack_kernel, in_specs=[pl.BlockSpec(memory_space=pltpu.HBM...  9.42 us
    all_to_all x1, waiting for transfers between devices, per_device(): sums = lax.all_to_all(message, ALL, 0, 0, tiled=True)  8.6 us
    pallas_call x1, Pallas kernels, tally(): pl.pallas_call(tally_kernel, out_shape=(jax.ShapeDtypeStruct((2, GROUP, 3...  7.32 us
    all_to_all x1, starting transfers between devices, per_device(): sums = lax.all_to_all(message, ALL, 0, 0, tiled=True)  4.38 us
  transfers between devices with their start and end apart: 1, of which 1 were waited for; matrix products, arithmetic and copies ran while one was open for 1% of the time, Pallas kernels for 0%

profile of v2, /device:TPU:1, one launch (start us, length us, event | category | flops | bytes accessed | tf_op | source)
XLA Modules:
  0.0 74.0 jit_solution(15462011370135402206)
XLA Ops:
  0.6 9.4 %pack.1 = f32[16,8,2,16,128]{4,3,2,1,0:T(8,128)} custom-call(s32[128,2048]{1,0:T(8,128)} %leaf_hbm.1, bf16[128,2048]{1,0:T(8,128)(2,1)} %oob_hbm.1, s32[1,2048]{1,0:T(1,128)} %bitcast.18), custom_call_target="tpu_custom_call" | custom-call | flops 40000000 | bytes 3700000 | tf_op jit(solution)/shard_map/pack/pallas_call | solution.py:167
  10.1 42.0 %all_to_all.16.in_ref = f32[128,2,16,128]{3,2,1,0:T(8,128)S(1)} all-to-all(f32[128,2,16,128]{3,2,1,0:T(8,128)} %bitcast.16), channel_id=1, replica_groups=mesh['rows_0'=4,'rows_1'=4,'trees_0'=4,'trees_1'=2] {'rows_0','rows_1','..., dimensions={0} | all-to-all | bytes 4194304 | tf_op jit(solution)/shard_map/all_to_all | solution.py:294
  52.0 7.3 %tally.1 = (f32[2,16,32,32]{3,2,1,0:T(8,128)S(1)}, f32[128,128]{1,0:T(8,128)}) custom-call(f32[128,2,16,128]{3,2,1,0:T(8,128)S(1)} %all_to_all.16.in_ref), custom_call_target="tpu_custom_call" | custom-call | flops 4000000000 | bytes 2500000 | tf_op jit(solution)/shard_map/tally/pallas_call | solution.py:253
  59.3 4.4 %all-to-all-start.1 = ((f32[128,1,128]{2,1,0:T(1,128)}), f32[128,1,128]{2,1,0:T(1,128)S(1)}, u32[]{:S(2)}, u32[]{:S(2)}) async-start(f32[128,1,128]{2,1,0:T(1,128)} %bitcast.5), calls=%async_computation.1 | async-start | bytes 131072 | tf_op jit(solution)/shard_map/all_to_all | solution.py:296
  63.7 0.2 reshape.28
  64.0 0.8 %copy.10 = f32[2,16,1024]{2,0,1:T(2,128)} copy(f32[2,16,1024]{2,1,0:T(8,128)S(1)} %reshape.28) | data formatting | bytes 262144 | tf_op jit(solution)/shard_map/reshape | solution.py:299
  64.7 8.6 %all-to-all-done.1 = f32[128,1,128]{2,1,0:T(1,128)S(1)} async-done(((f32[128,1,128]{2,1,0:T(1,128)}), f32[128,1,128]{2,1,0:T(1,128)S(1)}, u32[]{:S(2)}, u32[]{:S(2)}) %all-to-all-start.1) | async-done | bytes 65568 | tf_op jit(solution)/shard_map/all_to_all | solution.py:296
  73.3 0.6 errors.1
Async XLA Ops:
  59.3 14.0 %all-to-all-start.1 = ((f32[128,1,128]{2,1,0:T(1,128)}), f32[128,1,128]{2,1,0:T(1,128)S(1)}, u32[]{:S(2)}, u32[]{:S(2)}) async-start(f32[128,1,128]{2,1,0:T(1,128)} %bitcast.5), calls=%async_computation.1 | async-start | bytes 131072 | tf_op jit(solution)/shard_map/all_to_all | solution.py:296

commit v3 on v2

--- a/solution.py
+++ b/solution.py
@@ -83,7 +83,7 @@
             label = lab_ref[:, pl.ds(c * SPAN + q * 128, 128)].astype(F32)
             key = high + (code * 1024.0 + label)
             s_ref[pl.ds(c * SPAN + q * 128, 128), :] = jnp.transpose(key)
-        lax.fori_loop(c * SPAN // 256, (c + 1) * SPAN // 256, sort_32, 0)
+        lax.fori_loop(c * SPAN // 256, (c + 1) * SPAN // 256, sort_32, 0, unroll=True)
 
     def low_bits(b, carry):
         x = [get(b * 32 + r) for r in range(32)]
@@ -126,7 +126,7 @@
                 for d in reversed(range(k - 9)):
                     x = [across(v, swapped(v, 1 << d), 1 << d) for v in x]
             first = len(bits) - 2 if k <= 8 else len(bits) - 1
-            for d in reversed(range(first + 1)):
+            for d in reversed(range(1 if k == 11 else 0, first + 1)):
                 for e in range(2 * n):
                     if not e & (1 << d):
                         ordered(x, e, e | (1 << d))
@@ -134,11 +134,12 @@
                 put(v, val)
             return carry
 
-        lax.fori_loop(0, blocks * per_block, body, 0, unroll=UNROLL[k])
-
-    for k in range(6, 12):
+        lax.fori_loop(0, blocks * per_block, body, 0, unroll=True)
+
+    for k in range(6, 11):
         high_bits(k)
-        lax.fori_loop(0, REGS // 32, low_bits, 0)
+        lax.fori_loop(0, REGS // 32, low_bits, 0, unroll=True)
+    high_bits(11)
 
     def stored(p):
         return pltpu.make_async_copy(out_ref.at[p], out_hbm.at[p], out_sem.at[p])
@@ -158,9 +159,6 @@
         stored(p).start()
     for p in range(N_ROWS):
         stored(p).wait()
-
-
-UNROLL = {6: 4, 7: 2, 8: 1, 9: 1, 10: 1, 11: 1}
 
 
 def pack(leaf_index, out_of_bag, labels):
@@ -214,7 +212,7 @@
             lo_s[leaf, s] = lab2[leaf] - 32.0 * hi
         return carry
 
-    lax.fori_loop(0, HALF_DEV, spread, 0, unroll=4)
+    lax.fori_loop(0, HALF_DEV, spread, 0, unroll=True)
 
     def tree(t, carry):
         for leaf in range(2):
@@ -236,7 +234,7 @@
             top_s[leaf, pl.ds(t, 1), :] = jnp.max(table, axis=0, keepdims=True)
         return carry
 
-    lax.fori_loop(0, GROUP, tree, 0, unroll=4)
+    lax.fori_loop(0, GROUP, tree, 0, unroll=8)
     seen = jnp.zeros((GROUP, 1), F32)
     wrong = jnp.zeros((GROUP, 1), F32)
     for leaf in range(2):

time: 74.2 us -> 70.4 us (0.949)
  Pallas kernels: 17.4 us -> 13.5 us
    pallas_call x1, Pallas kernels: 9.42 us -> 6.88 us  [pack(): pl.pallas_call(pack_kernel, in_specs=[pl.BlockSpec(memory_space=pltpu.HBM...]
    pallas_call x1, Pallas kernels: 7.32 us -> 6.01 us  [tally(): pl.pallas_call(tally_kernel, out_shape=(jax.ShapeDtypeStruct((2, GROUP, 3...]
where the time goes in v3:
time: 70.4 us; the launch traced here: 70.1 us
  blocking collectives  42 us (60%)
  Pallas kernels  13.5 us (19%)
  waiting for transfers between devices  8.6 us (12%)
  starting transfers between devices  4.38 us (6%)
  local copies, waits for them, and re-layouts  0.99 us (1%)
    all_to_all x1, blocking collectives, per_device(): received = lax.all_to_all(packed, ALL, 0, 0, tiled=True)  42 us
    all_to_all x1, waiting for transfers between devices, per_device(): sums = lax.all_to_all(message, ALL, 0, 0, tiled=True)  8.6 us
    pallas_call x1, Pallas kernels, pack(): pl.pallas_call(pack_kernel, in_specs=[pl.BlockSpec(memory_space=pltpu.HBM...  6.88 us
    pallas_call x1, Pallas kernels, tally(): pl.pallas_call(tally_kernel, out_shape=(jax.ShapeDtypeStruct((2, GROUP, 3...  6.01 us
    all_to_all x1, starting transfers between devices, per_device(): sums = lax.all_to_all(message, ALL, 0, 0, tiled=True)  4.38 us
  transfers between devices with their start and end apart: 1, of which 1 were waited for; matrix products, arithmetic and copies ran while one was open for 1% of the time, Pallas kernels for 0%

profile of v3, /device:TPU:1, one launch (start us, length us, event | category | flops | bytes accessed | tf_op | source)
XLA Modules:
  0.0 70.1 jit_solution(12419139692925359110)
XLA Ops:
  0.6 6.9 %pack.1 = f32[16,8,2,16,128]{4,3,2,1,0:T(8,128)} custom-call(s32[128,2048]{1,0:T(8,128)} %leaf_hbm.1, bf16[128,2048]{1,0:T(8,128)(2,1)} %oob_hbm.1, s32[1,2048]{1,0:T(1,128)} %bitcast.18), custom_call_target="tpu_custom_call" | custom-call | flops 40000000 | bytes 3700000 | tf_op jit(solution)/shard_map/pack/pallas_call | solution.py:165
  7.5 42.0 %all_to_all.16.in_ref = f32[128,2,16,128]{3,2,1,0:T(8,128)S(1)} all-to-all(f32[128,2,16,128]{3,2,1,0:T(8,128)} %bitcast.16), channel_id=1, replica_groups=mesh['rows_0'=4,'rows_1'=4,'trees_0'=4,'trees_1'=2] {'rows_0','rows_1','..., dimensions={0} | all-to-all | bytes 4194304 | tf_op jit(solution)/shard_map/all_to_all | solution.py:292
  49.5 6.0 %tally.1 = (f32[2,16,32,32]{3,2,1,0:T(8,128)S(1)}, f32[128,128]{1,0:T(8,128)}) custom-call(f32[128,2,16,128]{3,2,1,0:T(8,128)S(1)} %all_to_all.16.in_ref), custom_call_target="tpu_custom_call" | custom-call | flops 4000000000 | bytes 2500000 | tf_op jit(solution)/shard_map/tally/pallas_call | solution.py:251
  55.5 4.4 %all-to-all-start.1 = ((f32[128,1,128]{2,1,0:T(1,128)}), f32[128,1,128]{2,1,0:T(1,128)S(1)}, u32[]{:S(2)}, u32[]{:S(2)}) async-start(f32[128,1,128]{2,1,0:T(1,128)} %bitcast.5), calls=%async_computation.1 | async-start | bytes 131072 | tf_op jit(solution)/shard_map/all_to_all | solution.py:294
  59.9 0.2 reshape.28
  60.1 0.8 %copy.10 = f32[2,16,1024]{2,0,1:T(2,128)} copy(f32[2,16,1024]{2,1,0:T(8,128)S(1)} %reshape.28) | data formatting | bytes 262144 | tf_op jit(solution)/shard_map/reshape | solution.py:297
  60.9 8.6 %all-to-all-done.1 = f32[128,1,128]{2,1,0:T(1,128)S(1)} async-done(((f32[128,1,128]{2,1,0:T(1,128)}), f32[128,1,128]{2,1,0:T(1,128)S(1)}, u32[]{:S(2)}, u32[]{:S(2)}) %all-to-all-start.1) | async-done | bytes 65568 | tf_op jit(solution)/shard_map/all_to_all | solution.py:294
  69.5 0.6 errors.1
Async XLA Ops:
  55.5 14.0 %all-to-all-start.1 = ((f32[128,1,128]{2,1,0:T(1,128)}), f32[128,1,128]{2,1,0:T(1,128)S(1)}, u32[]{:S(2)}, u32[]{:S(2)}) async-start(f32[128,1,128]{2,1,0:T(1,128)} %bitcast.5), calls=%async_computation.1 | async-start | bytes 131072 | tf_op jit(solution)/shard_map/all_to_all | solution.py:294

commit v4 on v3

v4 whole, which is shorter than its diff:
```python
import jax
import jax.numpy as jnp
from jax import lax
from jax.experimental import pallas as pl
from jax.experimental.pallas import tpu as pltpu
from jax.sharding import Mesh
from jax.sharding import PartitionSpec as P

CLASSES = 1000
LEAVES = 32
TREES_ALL = 128
ROW_DEV = 2048
N_DEV = 128
N_ROWS = 16
N_TREES = 8
GROUP = TREES_ALL // N_TREES
RANKS = ROW_DEV // LEAVES
ROWS = ("rows_0", "rows_1")
TREES = ("trees_0", "trees_1")
ALL = ROWS + TREES
REGS = ROW_DEV // 8
HALF_DEV = N_DEV // 2

F32 = jnp.float32
BF16 = jnp.bfloat16
I32 = jnp.int32


def ordered(x, i, j):
    x[i], x[j] = jnp.minimum(x[i], x[j]), jnp.maximum(x[i], x[j])


LEAF_STEP = float(1 << 20)


def sort_key(leaf_index, out_of_bag):
    w = out_of_bag.astype(F32) * 512.0
    code = jnp.minimum(jnp.minimum(w, w * 0.5 + 128.0), jnp.minimum(w * 0.25 + 256.0, w * 0.125 + 384.0))
    code = lax.optimization_barrier(code)
    return (leaf_index - 16).astype(F32) * LEAF_STEP + code * 1024.0


def pack_kernel(key_ref, lab_ref, out_ref, s_ref):
    sub = lax.broadcasted_iota(I32, (8, 128), 0)

    def get(v):
        return s_ref[pl.ds(pl.multiple_of(v * 8, 8), 8), :]

    def put(v, x):
        s_ref[pl.ds(pl.multiple_of(v * 8, 8), 8), :] = x

    def sort_32(b, carry):
        x = [get(b * 32 + r) for r in range(32)]
        for k in range(1, 6):
            for i in range(32):
                j = i ^ ((1 << k) - 1)
                if i < j:
                    ordered(x, i, j)
            for d in reversed(range(k - 1)):
                for i in range(32):
                    if not i & (1 << d):
                        ordered(x, i, i | (1 << d))
        for r in range(32):
            put(b * 32 + r, x[r])
        return carry

    for c in range(ROW_DEV // 128):
        cols = pl.ds(c * 128, 128)
        s_ref[cols, :] = jnp.transpose(key_ref[:, cols] + lab_ref[:, cols].astype(F32))
    lax.fori_loop(0, REGS // 32, sort_32, 0, unroll=True)

    def low_bits(b, carry):
        x = [get(b * 32 + r) for r in range(32)]
        for d in reversed(range(5)):
            for i in range(32):
                if not i & (1 << d):
                    ordered(x, i, i | (1 << d))
        for r in range(32):
            put(b * 32 + r, x[r])
        return carry

    def swapped(x, flip):
        return jnp.take_along_axis(x, sub ^ flip, axis=0, mode="promise_in_bounds")

    def across(x, y, bit):
        return jnp.where(sub & bit == 0, jnp.minimum(x, y), jnp.maximum(x, y))

    def high_bits(k):
        top = min(k, 8)
        bits = list(range(5, top))
        n = 1 << len(bits)
        per_block = 16
        blocks = REGS >> top

        def body(t, carry):
            block, low = t // per_block, t % per_block
            base = block << top
            at = [base + (h << 5) + low for h in range(n)] + [base + (h << 5) + (31 - low) for h in range(n)]
            x = [get(v) for v in at]
            mirror = lambda e: (n - 1 - e % n) + (n if e < n else 0)
            if k <= 8:
                for e in range(n):
                    if e & (n >> 1):
                        continue
                    ordered(x, e, mirror(e))
                    ordered(x, e + n, mirror(e + n))
            else:
                flip = (1 << (k - 8)) - 1
                x = [across(x[e], swapped(x[mirror(e)], flip), 1 << (k - 9)) for e in range(2 * n)]
                for d in reversed(range(k - 9)):
                    x = [across(v, swapped(v, 1 << d), 1 << d) for v in x]
            first = len(bits) - 2 if k <= 8 else len(bits) - 1
            for d in reversed(range(1 if k == 11 else 0, first + 1)):
                for e in range(2 * n):
                    if not e & (1 << d):
                        ordered(x, e, e | (1 << d))
            for v, val in zip(at, x):
                put(v, val)
            return carry

        lax.fori_loop(0, blocks * per_block, body, 0, unroll=True)

    for k in range(6, 11):
        high_bits(k)
        lax.fori_loop(0, REGS // 32, low_bits, 0, unroll=True)
    high_bits(11)

    odd = (lax.broadcasted_iota(I32, (1, 128), 1) >= RANKS).astype(F32)
    for p in range(N_ROWS):
        start = (p % 2) * 1024 + p // 2
        key = jnp.transpose(s_ref[pl.ds(start, 128, stride=8), :])
        rest = key - (odd + float(2 * p - 16)) * LEAF_STEP
        code = jnp.floor(rest * (1.0 / 1024.0))
        label = rest - code * 1024.0
        w = jnp.maximum(
            jnp.maximum(code, code * 2.0 - 256.0), jnp.maximum(code * 4.0 - 1024.0, code * 8.0 - 3072.0)
        ) * (1.0 / 512.0)
        out_ref[p, :, 0] = w.reshape(N_TREES, GROUP, 128)
        out_ref[p, :, 1] = label.reshape(N_TREES, GROUP, 128)


def pack(key, labels):
    return pl.pallas_call(
        pack_kernel,
        out_shape=jax.ShapeDtypeStruct((N_ROWS, N_TREES, 2, GROUP, 128), F32),
        scratch_shapes=[pltpu.VMEM((ROW_DEV, 128), F32)],
        compiler_params=pltpu.CompilerParams(vmem_limit_bytes=16 * 1024 * 1024),
        cost_estimate=pl.CostEstimate(flops=40_000_000, bytes_accessed=3_100_000, transcendentals=0),
        name="pack",
    )(key, labels.reshape(1, ROW_DEV))


def iota16(shape):
    return lax.broadcasted_iota(I32, shape, 0).astype(F32).astype(BF16)


TAG = 2 * GROUP


def tally_kernel(in_ref, tallies_ref, message_ref, w_s, hi_s, lo_s, flat_s, sum_s, top_s):
    low8 = lax.broadcasted_iota(I32, (8, 128), 1) < RANKS
    row16 = iota16((16, 128))
    quarter = lax.broadcasted_iota(I32, (32, 128), 0) % 4
    zero = jnp.zeros((16, 128), BF16)
    one = jnp.ones((16, 128), BF16)

    def halves(a, b):
        return (
            jnp.where(low8, a, pltpu.roll(b, RANKS, 1)),
            jnp.where(low8, pltpu.roll(a, RANKS, 1), b),
        )

    def spread(octet, s):
        trees = pl.ds(8 * octet, 8)
        w2 = halves(in_ref[s, 0, trees, :], in_ref[s + HALF_DEV, 0, trees, :])
        lab2 = halves(in_ref[s, 1, trees, :], in_ref[s + HALF_DEV, 1, trees, :])
        for leaf in range(2):
            hi = jnp.floor(lab2[leaf] * (1.0 / 32.0))
            w_s[octet, leaf, s] = w2[leaf]
            hi_s[octet, leaf, s] = hi
            lo_s[octet, leaf, s] = lab2[leaf] - 32.0 * hi

    def tree(t):
        octet, u = divmod(t, 8)
        for leaf in range(2):
            lhs, rhs = [], []
            for r in range(HALF_DEV):
                w_b = jnp.broadcast_to(w_s[octet, leaf, r, u : u + 1, :], (16, 128)).astype(BF16)
                hi_b = jnp.broadcast_to(hi_s[octet, leaf, r, u : u + 1, :], (16, 128)).astype(BF16)
                lo_b = jnp.broadcast_to(lo_s[octet, leaf, r, u : u + 1, :], (16, 128)).astype(BF16)
                lhs.append(jnp.concatenate([jnp.where(hi_b == row16 + 16 * i, w_b, zero) for i in range(2)], axis=0))
                rhs.append(jnp.concatenate([jnp.where(lo_b == row16 + 16 * i, one, zero) for i in range(2)], axis=0))
            table = lax.dot_general(
                jnp.concatenate(lhs, axis=1),
                jnp.concatenate(rhs, axis=1),
                (((1,), (1,)), ((), ())),
                preferred_element_type=F32,
            )
            sum_s[leaf, t : t + 1, :] = jnp.sum(table, axis=0, keepdims=True)
            top_s[leaf, t : t + 1, :] = jnp.max(table, axis=0, keepdims=True)
            wide = jnp.concatenate([table, jnp.zeros((32, 96), F32)], axis=1)
            placed = wide
            for j in range(1, 4):
                placed = jnp.where(quarter == j, pltpu.roll(wide, 32 * j, 1), placed)
            flat_s[t, leaf] = placed
            rows = flat_s[t, leaf, pl.ds(0, 8, stride=4), :]
            for j in range(1, 4):
                rows = rows + flat_s[t, leaf, pl.ds(j, 8, stride=4), :]
            for k in range(8):
                width = min(128, CLASSES - 128 * k)
                tallies_ref[t, leaf : leaf + 1, 128 * k : 128 * k + width] = rows[k : k + 1, :width]

    for s in range(HALF_DEV):
        spread(0, s)
    for t in range(8):
        for s in range(8 * t, 8 * t + 8):
            spread(1, s)
        tree(t)
    for t in range(8, GROUP):
        tree(t)
    seen = jnp.zeros((GROUP, 1), F32)
    wrong = jnp.zeros((GROUP, 1), F32)
    for leaf in range(2):
        total = jnp.sum(sum_s[leaf], axis=1, keepdims=True)
        seen = seen + total
        wrong = wrong + (total - jnp.max(top_s[leaf], axis=1, keepdims=True))
    lane = lax.broadcasted_iota(I32, (GROUP, 128), 1)
    row = lax.broadcasted_iota(I32, (GROUP, 128), 0)
    placed = jnp.where(lane == row, wrong, 0.0) + jnp.where(lane == row + GROUP, seen, 0.0)
    sums = jnp.broadcast_to(jnp.sum(placed, axis=0, keepdims=True), (N_DEV, 128))
    receiver = (lax.broadcasted_iota(I32, (N_DEV, 128), 0) % N_TREES).astype(F32)
    message_ref[...] = jnp.where(lax.broadcasted_iota(I32, (N_DEV, 128), 1) == TAG, receiver, sums)


def tally(received):
    return pl.pallas_call(
        tally_kernel,
        out_shape=(
            jax.ShapeDtypeStruct((GROUP, 2, CLASSES), F32),
            jax.ShapeDtypeStruct((N_DEV, 128), F32),
        ),
        scratch_shapes=[pltpu.VMEM((2, 2, HALF_DEV, 8, 128), F32)] * 3
        + [pltpu.VMEM((GROUP, 2, 32, 128), F32)]
        + [pltpu.VMEM((2, GROUP, 32), F32)] * 2,
        compiler_params=pltpu.CompilerParams(vmem_limit_bytes=16 * 1024 * 1024),
        cost_estimate=pl.CostEstimate(flops=4_000_000_000, bytes_accessed=2_500_000, transcendentals=0),
        name="tally",
    )(received)


def errors_kernel(in_ref, tree_ref, forest_ref):
    got = in_ref[...]
    source = (lax.broadcasted_iota(I32, (N_DEV, 128), 0) % N_TREES).astype(F32)
    mine = jnp.sum(jnp.where(source == got[:, TAG : TAG + 1], got, 0.0), axis=0, keepdims=True)
    every = jnp.sum(got, axis=0, keepdims=True)
    lane = lax.broadcasted_iota(I32, (1, 128), 1)
    wrong = jnp.sum(jnp.where(lane < GROUP, every, 0.0), axis=1, keepdims=True)
    seen = jnp.sum(jnp.where((lane >= GROUP) & (lane < 2 * GROUP), every, 0.0), axis=1, keepdims=True)
    ratio = mine / pltpu.roll(mine, 128 - GROUP, 1)
    tree_ref[...] = ratio[:, :GROUP]
    forest_ref[...] = wrong / seen


def errors(received):
    return pl.pallas_call(
        errors_kernel,
        out_shape=(
            jax.ShapeDtypeStruct((1, GROUP), F32),
            jax.ShapeDtypeStruct((1, 1), F32),
        ),
        compiler_params=pltpu.CompilerParams(vmem_limit_bytes=4 * 1024 * 1024),
        name="errors",
    )(received)


def per_device(leaf_index, out_of_bag, labels):
    packed = pack(sort_key(leaf_index, out_of_bag), labels).reshape(N_DEV, 2, GROUP, 128)
    received = lax.all_to_all(packed, ALL, 0, 0, tiled=True)
    tallies, message = tally(received)
    sums = lax.all_to_all(message, ALL, 0, 0, tiled=True)
    tree_error, forest_error = errors(sums)
    return tallies, tree_error.reshape(GROUP), forest_error.reshape(())


def solution(mesh):
    split = Mesh(mesh.devices.reshape(4, 4, 4, 2), ALL)
    return jax.shard_map(
        per_device,
        mesh=split,
        in_specs=(P(None, ALL), P(None, ALL), P(ALL)),
        out_specs=(P(TREES, ROWS, None), P(TREES), P()),
        check_vma=False,
    )
```

time: 70.4 us -> 67.9 us (0.964)
  blocking collectives: 42 us -> 55.5 us
  waiting for transfers between devices: 8.6 us -> 0 us
  starting transfers between devices: 4.38 us -> 0 us
  Pallas kernels: 13.5 us -> 9.89 us
  other arithmetic: 0 us -> 1.68 us
  local copies, waits for them, and re-layouts: 0.99 us -> 0.01 us
    all_to_all x0 -> x1, blocking collectives: none -> 13.7 us  [per_device(): sums = lax.all_to_all(message, ALL, 0, 0, tiled=True)]
    all_to_all x1 -> x0, waiting for transfers between devices: 8.6 us -> none  [per_device(): sums = lax.all_to_all(message, ALL, 0, 0, tiled=True)]
    all_to_all x1 -> x0, starting transfers between devices: 4.38 us -> none  [per_device(): sums = lax.all_to_all(message, ALL, 0, 0, tiled=True)]
    pallas_call x3, Pallas kernels: 13.5 us -> 9.89 us  [the longest x1 5.6 us: tally(): pl.pallas_call(tally_kernel, out_shape=(jax.ShapeDtypeStruct((GROUP, 2, C...]
    min x0 -> x1, other arithmetic: none -> 1.5 us  [sort_key(): jnp.minimum(jnp.minimum(w, w * 0.5 + 128.0), jnp.minimum(w * 0.25 + 256.0...]
    reshape x2 -> x0, local copies, waits for them, and re-layouts: 0.99 us -> none  [per_device(): tallies = jnp.swapaxes(table.reshape(2, GROUP, 1024), 0, 1)[:, :, :CLASSES]]
  transfers between devices with their start and end apart: 1 -> 0, of which waited for: 1 -> 0; matrix products, arithmetic and copies ran while one was open for 1% -> 0% of each run, Pallas kernels for 0% -> 0%
where the time goes in v4:
time: 67.9 us; the launch traced here: 67.7 us
  blocking collectives  55.5 us (82%)
  Pallas kernels  9.89 us (15%)
  other arithmetic  1.68 us (2%)
  between operations  0.68 us (1%)
    all_to_all x1, blocking collectives, per_device(): received = lax.all_to_all(packed, ALL, 0, 0, tiled=True)  41.8 us
    all_to_all x1, blocking collectives, per_device(): sums = lax.all_to_all(message, ALL, 0, 0, tiled=True)  13.7 us
    pallas_call x1, Pallas kernels, tally(): pl.pallas_call(tally_kernel, out_shape=(jax.ShapeDtypeStruct((GROUP, 2, C...  5.6 us
    pallas_call x1, Pallas kernels, pack(): pl.pallas_call(pack_kernel, out_shape=jax.ShapeDtypeStruct((N_ROWS, N_TRE...  3.59 us
    min x1, other arithmetic, sort_key(): jnp.minimum(jnp.minimum(w, w * 0.5 + 128.0), jnp.minimum(w * 0.25 + 256.0...  1.5 us

profile of v4, /device:TPU:1, one launch (start us, length us, event | category | flops | bytes accessed | tf_op | source)
XLA Modules:
  0.0 67.7 jit_solution(1640884585462640255)
XLA Ops:
  0.6 0.0 copy-start.1
  0.6 0.0 copy-start
  0.7 1.5 %fusion.1 = f32[128,2048]{1,0:T(8,128)S(1)} fusion(bf16[128,2048]{1,0:T(8,128)(2,1)} %param.4), kind=kLoop, calls=%fused_computation.5 | loop fusion | flops 2883584 | bytes 1572864 | tf_op jit(solution)/shard_map/min | solution.py:38
  2.2 0.0 copy-done.1
  2.2 0.2 multiply_add_fusion.key_ref
  2.4 0.0 copy-done
  2.4 3.6 %pack.1 = f32[16,8,2,16,128]{4,3,2,1,0:T(8,128)S(1)} custom-call(f32[128,2048]{1,0:T(8,128)S(1)} %multiply_add_fusion.key_ref, s32[1,2048]{1,0:T(1,128)S(1)} %bitcast.11), custom_call_target="tpu_custom_call" | custom-call | flops 40000000 | bytes 3100000 | tf_op jit(solution)/shard_map/pack/pallas_call | solution.py:143
  6.0 41.8 %all_to_all.16.in_ref = f32[128,2,16,128]{3,2,1,0:T(8,128)S(1)} all-to-all(f32[128,2,16,128]{3,2,1,0:T(8,128)S(1)} %bitcast.8), channel_id=1, replica_groups=mesh['rows_0'=4,'rows_1'=4,'trees_0'=4,'trees_1'=2] {'rows_0','rows_1','..., dimensions={0} | all-to-all | bytes 4194304 | tf_op jit(solution)/shard_map/all_to_all | solution.py:278
  47.7 5.6 %tally.1 = (f32[16,2,1000]{2,1,0:T(2,128)}, f32[128,128]{1,0:T(8,128)S(1)}) custom-call(f32[128,2,16,128]{3,2,1,0:T(8,128)S(1)} %all_to_all.16.in_ref), custom_call_target="tpu_custom_call" | custom-call | flops 4000000000 | bytes 2500000 | tf_op jit(solution)/shard_map/tally/pallas_call | solution.py:236
  53.3 13.7 %all_to_all.17 = f32[128,1,128]{2,1,0:T(1,128)S(1)} all-to-all(f32[128,1,128]{2,1,0:T(1,128)S(1)} %bitcast.10), channel_id=1, replica_groups=mesh['rows_0'=4,'rows_1'=4,'trees_0'=4,'trees_1'=2] {'rows_0','rows_1','..., dimensions={0} | all-to-all | bytes 131072 | tf_op jit(solution)/shard_map/all_to_all | solution.py:280
  67.0 0.7 %errors.1 = (f32[1,16]{1,0:T(1,128)}, f32[1,1]{1,0:T(1,128)}) custom-call(f32[128,128]{1,0:T(8,128)S(1)} %bitcast.9), custom_call_target="tpu_custom_call" | custom-call | tf_op jit(solution)/shard_map/errors/pallas_call | solution.py:265
Async XLA Ops:
  0.6 1.5 %copy-start.1 = (s32[128,2048]{1,0:T(8,128)S(1)}, s32[128,2048]{1,0:T(8,128)}, u32[]{:S(2)}) copy-start(s32[128,2048]{1,0:T(8,128)} %param.3) | copy-start | bytes 3145732
  0.6 1.7 %copy-start = (s32[2048]{0:T(1024)S(1)}, s32[2048]{0:T(1024)}, u32[]{:S(2)}) copy-start(s32[2048]{0:T(1024)} %param.5) | copy-start | bytes 24580

commit v5 on v4

--- a/solution.py
+++ b/solution.py
@@ -248,7 +248,8 @@
     )(received)
 
 
-def errors_kernel(in_ref, tree_ref, forest_ref):
+def errors_kernel(in_ref, made_ref, tallies_ref, tree_ref, forest_ref):
+    tallies_ref[...] = made_ref[...]
     got = in_ref[...]
     source = (lax.broadcasted_iota(I32, (N_DEV, 128), 0) % N_TREES).astype(F32)
     mine = jnp.sum(jnp.where(source == got[:, TAG : TAG + 1], got, 0.0), axis=0, keepdims=True)
@@ -261,16 +262,17 @@
     forest_ref[...] = wrong / seen
 
 
-def errors(received):
+def errors(received, tallies):
     return pl.pallas_call(
         errors_kernel,
         out_shape=(
+            jax.ShapeDtypeStruct((GROUP, 2, CLASSES), F32),
             jax.ShapeDtypeStruct((1, GROUP), F32),
             jax.ShapeDtypeStruct((1, 1), F32),
         ),
         compiler_params=pltpu.CompilerParams(vmem_limit_bytes=4 * 1024 * 1024),
         name="errors",
-    )(received)
+    )(received, tallies)
 
 
 def per_device(leaf_index, out_of_bag, labels):
@@ -278,7 +280,7 @@
     received = lax.all_to_all(packed, ALL, 0, 0, tiled=True)
     tallies, message = tally(received)
     sums = lax.all_to_all(message, ALL, 0, 0, tiled=True)
-    tree_error, forest_error = errors(sums)
+    tallies, tree_error, forest_error = errors(sums, tallies)
     return tallies, tree_error.reshape(GROUP), forest_error.reshape(())
 
 

time: 67.9 us -> 67.3 us (level)
  no operation moved by 1% of the time
where the time goes in v5:
time: 67.3 us; the launch traced here: 67.1 us
  blocking collectives  55.5 us (82%)
  Pallas kernels  9.3 us (14%)
  other arithmetic  1.68 us (2%)
  between operations  0.69 us (1%)
    all_to_all x1, blocking collectives, per_device(): received = lax.all_to_all(packed, ALL, 0, 0, tiled=True)  41.8 us
    all_to_all x1, blocking collectives, per_device(): sums = lax.all_to_all(message, ALL, 0, 0, tiled=True)  13.7 us
    pallas_call x1, Pallas kernels, tally(): pl.pallas_call(tally_kernel, out_shape=(jax.ShapeDtypeStruct((GROUP, 2, C...  4.94 us
    pallas_call x1, Pallas kernels, pack(): pl.pallas_call(pack_kernel, out_shape=jax.ShapeDtypeStruct((N_ROWS, N_TRE...  3.59 us
    min x1, other arithmetic, sort_key(): jnp.minimum(jnp.minimum(w, w * 0.5 + 128.0), jnp.minimum(w * 0.25 + 256.0...  1.5 us

profile of v5, /device:TPU:1, one launch (start us, length us, event | category | flops | bytes accessed | tf_op | source)
XLA Modules:
  0.0 67.1 jit_solution(13224619263952745835)
XLA Ops:
  0.6 0.0 copy-start.1
  0.6 0.0 copy-start
  0.7 1.5 %fusion.1 = f32[128,2048]{1,0:T(8,128)S(1)} fusion(bf16[128,2048]{1,0:T(8,128)(2,1)} %param.4), kind=kLoop, calls=%fused_computation.5 | loop fusion | flops 2883584 | bytes 1572864 | tf_op jit(solution)/shard_map/min | solution.py:38
  2.2 0.0 copy-done.1
  2.2 0.2 multiply_add_fusion.key_ref
  2.4 0.0 copy-done
  2.4 3.6 %pack.1 = f32[16,8,2,16,128]{4,3,2,1,0:T(8,128)S(1)} custom-call(f32[128,2048]{1,0:T(8,128)S(1)} %multiply_add_fusion.key_ref, s32[1,2048]{1,0:T(1,128)S(1)} %bitcast.11), custom_call_target="tpu_custom_call" | custom-call | flops 40000000 | bytes 3100000 | tf_op jit(solution)/shard_map/pack/pallas_call | solution.py:143
  6.0 41.8 %all_to_all.16.in_ref = f32[128,2,16,128]{3,2,1,0:T(8,128)S(1)} all-to-all(f32[128,2,16,128]{3,2,1,0:T(8,128)S(1)} %bitcast.8), channel_id=1, replica_groups=mesh['rows_0'=4,'rows_1'=4,'trees_0'=4,'trees_1'=2] {'rows_0','rows_1','..., dimensions={0} | all-to-all | bytes 4194304 | tf_op jit(solution)/shard_map/all_to_all | solution.py:280
  47.7 4.9 %tally.1 = (f32[16,2,1000]{2,1,0:T(2,128)S(1)}, f32[128,128]{1,0:T(8,128)S(1)}) custom-call(f32[128,2,16,128]{3,2,1,0:T(8,128)S(1)} %all_to_all.16.in_ref), custom_call_target="tpu_custom_call" | custom-call | flops 4000000000 | bytes 2500000 | tf_op jit(solution)/shard_map/tally/pallas_call | solution.py:236
  52.7 13.7 %all_to_all.17 = f32[128,1,128]{2,1,0:T(1,128)S(1)} all-to-all(f32[128,1,128]{2,1,0:T(1,128)S(1)} %bitcast.10), channel_id=1, replica_groups=mesh['rows_0'=4,'rows_1'=4,'trees_0'=4,'trees_1'=2] {'rows_0','rows_1','..., dimensions={0} | all-to-all | bytes 131072 | tf_op jit(solution)/shard_map/all_to_all | solution.py:282
  66.4 0.8 %errors.1 = (f32[16,2,1000]{2,1,0:T(2,128)}, f32[1,16]{1,0:T(1,128)}, f32[1,1]{1,0:T(1,128)}) custom-call(f32[128,128]{1,0:T(8,128)S(1)} %bitcast.9, f32[16,2,1000]{2,1,0:T(2,128)S(1)} %get-tuple-element.9.made_ref), custom_call_target="tpu_custom_call" | custom-call | tf_op jit(solution)/shard_map/errors/pallas_call | solution.py:266
Async XLA Ops:
  0.6 1.5 %copy-start.1 = (s32[128,2048]{1,0:T(8,128)S(1)}, s32[128,2048]{1,0:T(8,128)}, u32[]{:S(2)}) copy-start(s32[128,2048]{1,0:T(8,128)} %param.3) | copy-start | bytes 3145732
  0.6 1.7 %copy-start = (s32[2048]{0:T(1024)S(1)}, s32[2048]{0:T(1024)}, u32[]{:S(2)}) copy-start(s32[2048]{0:T(1024)} %param.5) | copy-start | bytes 24580

commit v6 on v5

--- a/solution.py
+++ b/solution.py
@@ -26,6 +26,19 @@
 I32 = jnp.int32
 
 
+def odd_even(n):
+    p = 1
+    while p < n:
+        k = p
+        while k:
+            for j in range(k % p, n - k, 2 * k):
+                for i in range(min(k, n - j - k)):
+                    if (i + j) // (2 * p) == (i + j + k) // (2 * p):
+                        yield i + j, i + j + k
+            k //= 2
+        p *= 2
+
+
 def ordered(x, i, j):
     x[i], x[j] = jnp.minimum(x[i], x[j]), jnp.maximum(x[i], x[j])
 
@@ -51,15 +64,8 @@
 
     def sort_32(b, carry):
         x = [get(b * 32 + r) for r in range(32)]
-        for k in range(1, 6):
-            for i in range(32):
-                j = i ^ ((1 << k) - 1)
-                if i < j:
-                    ordered(x, i, j)
-            for d in reversed(range(k - 1)):
-                for i in range(32):
-                    if not i & (1 << d):
-                        ordered(x, i, i | (1 << d))
+        for i, j in odd_even(32):
+            ordered(x, i, j)
         for r in range(32):
             put(b * 32 + r, x[r])
         return carry

time: 67.3 us -> 67.2 us (level)
  no operation moved by 1% of the time
where the time goes in v6:
time: 67.2 us; the launch traced here: 67 us
  blocking collectives  55.5 us (83%)
  Pallas kernels  9.2 us (14%)
  other arithmetic  1.68 us (2%)
  between operations  0.69 us (1%)
    all_to_all x1, blocking collectives, per_device(): received = lax.all_to_all(packed, ALL, 0, 0, tiled=True)  41.8 us
    all_to_all x1, blocking collectives, per_device(): sums = lax.all_to_all(message, ALL, 0, 0, tiled=True)  13.7 us
    pallas_call x1, Pallas kernels, tally(): pl.pallas_call(tally_kernel, out_shape=(jax.ShapeDtypeStruct((GROUP, 2, C...  4.94 us
    pallas_call x1, Pallas kernels, pack(): pl.pallas_call(pack_kernel, out_shape=jax.ShapeDtypeStruct((N_ROWS, N_TRE...  3.49 us
    min x1, other arithmetic, sort_key(): jnp.minimum(jnp.minimum(w, w * 0.5 + 128.0), jnp.minimum(w * 0.25 + 256.0...  1.5 us

profile of v6, /device:TPU:1, one launch (start us, length us, event | category | flops | bytes accessed | tf_op | source)
XLA Modules:
  0.0 67.0 jit_solution(5893453744487726760)
XLA Ops:
  0.6 0.0 copy-start.1
  0.6 0.0 copy-start
  0.7 1.5 %fusion.1 = f32[128,2048]{1,0:T(8,128)S(1)} fusion(bf16[128,2048]{1,0:T(8,128)(2,1)} %param.4), kind=kLoop, calls=%fused_computation.5 | loop fusion | flops 2883584 | bytes 1572864 | tf_op jit(solution)/shard_map/min | solution.py:51
  2.2 0.0 copy-done.1
  2.2 0.2 multiply_add_fusion.key_ref
  2.4 0.0 copy-done
  2.4 3.5 %pack.1 = f32[16,8,2,16,128]{4,3,2,1,0:T(8,128)S(1)} custom-call(f32[128,2048]{1,0:T(8,128)S(1)} %multiply_add_fusion.key_ref, s32[1,2048]{1,0:T(1,128)S(1)} %bitcast.11), custom_call_target="tpu_custom_call" | custom-call | flops 40000000 | bytes 3100000 | tf_op jit(solution)/shard_map/pack/pallas_call | solution.py:149
  5.9 41.8 %all_to_all.16.in_ref = f32[128,2,16,128]{3,2,1,0:T(8,128)S(1)} all-to-all(f32[128,2,16,128]{3,2,1,0:T(8,128)S(1)} %bitcast.8), channel_id=1, replica_groups=mesh['rows_0'=4,'rows_1'=4,'trees_0'=4,'trees_1'=2] {'rows_0','rows_1','..., dimensions={0} | all-to-all | bytes 4194304 | tf_op jit(solution)/shard_map/all_to_all | solution.py:286
  47.6 4.9 %tally.1 = (f32[16,2,1000]{2,1,0:T(2,128)S(1)}, f32[128,128]{1,0:T(8,128)S(1)}) custom-call(f32[128,2,16,128]{3,2,1,0:T(8,128)S(1)} %all_to_all.16.in_ref), custom_call_target="tpu_custom_call" | custom-call | flops 4000000000 | bytes 2500000 | tf_op jit(solution)/shard_map/tally/pallas_call | solution.py:242
  52.6 13.7 %all_to_all.17 = f32[128,1,128]{2,1,0:T(1,128)S(1)} all-to-all(f32[128,1,128]{2,1,0:T(1,128)S(1)} %bitcast.10), channel_id=1, replica_groups=mesh['rows_0'=4,'rows_1'=4,'trees_0'=4,'trees_1'=2] {'rows_0','rows_1','..., dimensions={0} | all-to-all | bytes 131072 | tf_op jit(solution)/shard_map/all_to_all | solution.py:288
  66.3 0.8 %errors.1 = (f32[16,2,1000]{2,1,0:T(2,128)}, f32[1,16]{1,0:T(1,128)}, f32[1,1]{1,0:T(1,128)}) custom-call(f32[128,128]{1,0:T(8,128)S(1)} %bitcast.9, f32[16,2,1000]{2,1,0:T(2,128)S(1)} %get-tuple-element.9.made_ref), custom_call_target="tpu_custom_call" | custom-call | tf_op jit(solution)/shard_map/errors/pallas_call | solution.py:272
Async XLA Ops:
  0.6 1.5 %copy-start.1 = (s32[128,2048]{1,0:T(8,128)S(1)}, s32[128,2048]{1,0:T(8,128)}, u32[]{:S(2)}) copy-start(s32[128,2048]{1,0:T(8,128)} %param.3) | copy-start | bytes 3145732
  0.6 1.7 %copy-start = (s32[2048]{0:T(1024)S(1)}, s32[2048]{0:T(1024)}, u32[]{:S(2)}) copy-start(s32[2048]{0:T(1024)} %param.5) | copy-start | bytes 24580
